TPU v7x, 32 devices: a whole 2x2x4 slice. The times are simulated.
32 devices in a mesh: mem: 4 (over x, core), reg: 8 (over z, y).
Axes of the slice: x: 2, y: 2, z: 4, core: 2. Of those that a mesh axis runs over, the one named last changes fastest.
Arguments:
- profiles: bfloat16 [2048, 80, 127], P('reg', 'mem'), may hold values from -6 to 6
- jacobian: bfloat16 [2048, 16, 127], P('reg'), may hold values from -0.5 to 0.5
- departure: float32 [32768], P('reg'), may hold values from -6 to 6
- obs_rinv: float32 [32768], P('reg'), may hold values from 0.1 to 2
- obs_level: int32 [32768], P('reg'), may hold values from 0 to 126
- vertical_modes: float32 [127, 12], replicated, may hold values from -2 to 2
- send_rows: int32 [8, 7, 512], P('reg'), may hold values from -1 to 4095, as said below
- counts: int32 [8, 7], P('reg'), may hold values from 64 to 512, as said below
- loc_taper: float32 [8, 7, 512], P('reg'), may hold values from 0.05 to 1
Outputs:
- gram_matrices: float32 [8, 960, 960], P('reg', 'mem')
- weighted_departures: float32 [8, 960], P('reg', 'mem')
Inputs may be any that keep to these rules, and one draw needn't show every extreme that they name: counts[s, d] of the 512 slots that owner s sends to region (s + d - 3) mod 8 are live, the first ones; in every draw one region has all 512 slots live from each of its 7 owners. `send_rows`: a live slot holds a row of the owner's 4096 observations, no row twice within one (s, d); the other slots hold -1.
All inputs are finite; a program needn't handle non-finite values.
Results may differ from a plain program's by a relative error of at most 0.0095.
Values may be sent and summed in bfloat16 or wider, within the bound.
A program may use at most 64 MiB of HBM per device.

v0:
```python
import jax
import jax.numpy as jnp
from jax import lax
from jax.sharding import PartitionSpec as P

ENS = 80


def from_behind(block, axis, distance):
    devices = range(lax.axis_size(axis))
    route = [((i - distance) % len(devices), i) for i in devices]
    return lax.ppermute(block, axis, route)


def local(
    profiles, jacobian, departure, obs_rinv, obs_level, vertical_modes, send_rows, counts, loc_taper
):
    members = profiles.shape[1]
    levels = profiles.shape[2]
    blocks = send_rows.shape[1]
    middle = blocks // 2
    capacity = send_rows.shape[2]
    all_slots = blocks * capacity
    factor = (ENS - 1) ** (-0.5)
    perturbed = jnp.einsum("cql,cml->cqm", jacobian, profiles, preferred_element_type=jnp.float32)
    perturbed = perturbed.reshape(-1, members).astype(jnp.bfloat16)
    table = jnp.concatenate(
        [
            perturbed.astype(jnp.float32),
            obs_rinv[:, None],
            departure[:, None],
            obs_level.astype(jnp.float32)[:, None],
        ],
        axis=1,
    )
    live_slot = lax.broadcasted_iota(jnp.int32, (blocks, capacity), 1) < counts[0][:, None]
    picked = jnp.where(live_slot, send_rows[0], 0).reshape(-1)
    table_rows = jnp.take(table, picked, axis=0)
    chosen = table_rows[:, :members].T.astype(jnp.bfloat16)
    slot_rinv = table_rows[:, members]
    slot_departure = table_rows[:, members + 1]
    slot_level = table_rows[:, members + 2].astype(jnp.int32)
    weight32 = jnp.where(live_slot.reshape(-1), slot_rinv * loc_taper[0].reshape(-1), 0.0)
    weight = weight32.astype(jnp.bfloat16)
    dep_weighted = (weight32 * slot_departure).astype(jnp.bfloat16)
    one_hot = (
        lax.broadcasted_iota(jnp.int32, (levels, all_slots), 0) == slot_level[None, :]
    ).astype(jnp.float32)
    mode_values = (
        jnp.dot(vertical_modes.T, one_hot, precision=lax.Precision.HIGHEST) * factor
    ).astype(jnp.bfloat16)
    side_rows = jnp.concatenate([weight[None, :], dep_weighted[None, :], mode_values], axis=0)
    row_pieces = []
    side_pieces = []
    for offset in range(blocks):
        first_slot = offset * capacity
        block_rows = chosen[:, first_slot : first_slot + capacity]
        block_side = side_rows[:, first_slot : first_slot + capacity]
        if offset != middle:
            block_rows, block_side = from_behind((block_rows, block_side), "reg", offset - middle)
        row_pieces.append(block_rows)
        side_pieces.append(block_side)
    region_pert = jnp.concatenate(row_pieces, axis=1)
    region_side = jnp.concatenate(side_pieces, axis=1)
    mem_index = lax.axis_index("mem")
    region_pert = lax.all_gather(region_pert, "mem", axis=0, tiled=True)
    slot_weight = region_side[0]
    slot_dep = region_side[1]
    slot_modes = region_side[2:]
    modulated = region_pert[:, None, :] * slot_modes[None, :, :]
    modulated = modulated.reshape(-1, region_pert.shape[1])
    weighted = modulated * slot_weight[None, :]
    contract = (((1,), (1,)), ((), ()))
    own_count = members * vertical_modes.shape[1]
    own_rows = lax.dynamic_slice_in_dim(modulated, mem_index * own_count, own_count, 0)
    gram_block = lax.dot_general(own_rows, weighted, contract, preferred_element_type=jnp.float32)
    dep_block = jnp.dot(own_rows, slot_dep, preferred_element_type=jnp.float32)
    return (gram_block[None], dep_block[None])


def solution(mesh):
    in_specs = (
        P("reg", "mem", None),
        P("reg", None, None),
        P("reg"),
        P("reg"),
        P("reg"),
        P(),
        P("reg", None, None),
        P("reg", None),
        P("reg", None, None),
    )
    out_specs = (P("reg", "mem", None), P("reg", "mem"))
    return jax.shard_map(local, mesh=mesh, in_specs=in_specs, out_specs=out_specs, check_vma=False)
```

profile of v0, /device:TPU:0, one launch (start us, length us, event | category | flops | bytes accessed | tf_op | source)
XLA Modules:
  0.0 96.1 jit_solution(7590952081994285337)
XLA Ops:
  0.6 0.0 copy-start
  0.6 0.8 iota_compare_fusion.2
  1.5 0.8 fusion.21
  2.3 2.5 %copy.30 = bf16[256,16,127]{2,1,0:T(8,128)(2,1)S(1)} copy(bf16[256,16,127]{0,1,2:T(8,128)(2,1)} %param.10) | data formatting | bytes 2080768 | tf_op args[1]
  4.8 0.0 copy-done
  4.8 0.9 fusion.11
  5.8 0.0 copy-start.2
  5.8 1.6 %bitcast_convert_fusion = f32[4096,20]{1,0:T(8,128)} fusion(bf16[256,16,20]{2,1,0:T(8,128)(2,1)S(1)} %fusion.11), kind=kLoop, calls=%fused_computation.22 | loop fusion | flops 81920 | bytes 491520 | tf_op jit(solution)/shard_map/convert_element_type | solution.py:29
  7.4 0.0 copy-done.4
  7.4 2.0 %copy.34 = f32[4096,1]{1,0:T(8,128)} copy(f32[4096,1]{0,1:T(1,128)S(1)} %bitcast.33) | data formatting | bytes 32768 | tf_op jit(solution)/shard_map/broadcast_in_dim | solution.py:32
  9.4 0.0 copy-done.2
  9.4 2.0 %copy.32 = f32[4096,1]{1,0:T(8,128)} copy(f32[4096,1]{0,1:T(1,128)S(1)} %bitcast.35) | data formatting | bytes 32768 | tf_op jit(solution)/shard_map/broadcast_in_dim | solution.py:30
  11.4 0.0 copy-done.3
  11.4 2.0 %copy.33 = f32[4096,1]{1,0:T(8,128)} copy(f32[4096,1]{0,1:T(1,128)S(1)} %bitcast.36) | data formatting | bytes 32768 | tf_op jit(solution)/shard_map/broadcast_in_dim | solution.py:31
  13.4 5.2 %pad_maximum_fusion = f32[4096,23]{1,0:T(8,128)S(1)} fusion(f32[4096,1]{1,0:T(8,128)} %copy.34, f32[4096,1]{1,0:T(8,128)} %copy.33, f32[4096,1]{1,0:T(8,128)} %copy.32, f32[4096,20]{1,0:T(8,128)} %bitcast_convert_fusion), kind=kLoop, calls=%fused_computation.8 | loop fusion | flops 282624 | bytes 753664 | tf_op jit(solution)/shard_map/concatenate | solution.py:27
  18.6 7.4 %gather_fusion = f32[3584,23]{1,0:T(8,128)} fusion(f32[4096,23]{1,0:T(8,128)S(1)} %pad_maximum_fusion, s32[4096]{0:T(1024)S(1)} %pad_clamp_fusion), kind=kCustom, calls=%fused_computation | custom fusion | bytes 673792 | tf_op jit(solution)/shard_map/jit(_take)/gather | solution.py:38
  25.9 3.0 %broadcast_select_fusion = f32[3584,23]{1,0:T(8,128)S(1)} fusion(f32[3584,23]{1,0:T(8,128)} %gather_fusion, pred[3584]{0:T(1024)(128)(4,1)S(1)} %compare_and_fusion), kind=kLoop, calls=%fused_computation.25 | loop fusion | flops 82432 | bytes 663040 | tf_op jit(solution)/shard_map/jit(_take)/select_n | solution.py:38
  28.9 0.0 copy-start.5
  28.9 0.0 copy-start.6
  29.0 2.0 %slice_reduce_fusion = (f32[3584]{0:T(1024)S(1)}, f32[3584]{0:T(1024)S(1)}) fusion(f32[3584,23]{1,0:T(8,128)S(1)} %broadcast_select_fusion), kind=kLoop, calls=%fused_computation.11 | loop fusion | bytes 57344 | tf_op jit(solution)/shard_map/slice | solution.py:41
  30.9 1.0 %fusion.5 = s32[3584]{0:T(1024)S(1)} fusion(f32[3584,23]{1,0:T(8,128)S(1)} %broadcast_select_fusion), kind=kLoop, calls=%fused_computation.10 | loop fusion | flops 3584 | bytes 28672 | tf_op jit(solution)/shard_map/convert_element_type | solution.py:42
  32.1 0.0 copy-done.6
  32.1 0.7 fusion.3
  32.8 0.1 pad_maximum_fusion.1
  32.9 5.1 %collective-permute-start.6 = (bf16[14,512]{1,0:T(8,128)(2,1)S(1)}, bf16[14,512]{1,0:T(8,128)(2,1)S(1)}, u32[]{:S(2)}, u32[]{:S(2)}) collective-permute-start(bf16[14,512]{1,0:T(8,128)(2,1)S(1)} %get-tuple-element.19), channel_id=1, source_target_pairs={{3,0},{4,1},{5,2},{6,3},{7,4},{0,5},{1,6},{2,7},{11,8},{12,9},{13,... | collective-permute-start | bytes 43016 | tf_op jit(solution)/shard_map/ppermute | solution.py:12
  38.0 1.3 %collective-permute-start.7 = (bf16[14,512]{1,0:T(8,128)(2,1)S(1)}, bf16[14,512]{1,0:T(8,128)(2,1)S(1)}, u32[]{:S(2)}, u32[]{:S(2)}) collective-permute-start(bf16[14,512]{1,0:T(8,128)(2,1)S(1)} %get-tuple-element.18), channel_id=1, source_target_pairs={{2,0},{3,1},{4,2},{5,3},{6,4},{7,5},{0,6},{1,7},{10,8},{11,9},{12,... | collective-permute-start | bytes 43016 | tf_op jit(solution)/shard_map/ppermute | solution.py:12
  39.3 0.5 collective-permute-start.8
  39.8 0.1 fusion.19
  39.9 0.1 fusion.26
  40.0 2.7 %collective-permute-start = (bf16[20,512]{0,1:T(8,128)(2,1)S(1)}, bf16[20,512]{0,1:T(8,128)(2,1)S(1)}, u32[]{:S(2)}, u32[]{:S(2)}) collective-permute-start(bf16[20,512]{0,1:T(8,128)(2,1)S(1)} %get-tuple-element.12), channel_id=1, source_target_pairs={{3,0},{4,1},{5,2},{6,3},{7,4},{0,5},{1,6},{2,7},{11,8},{12,9},{13,... | collective-permute-start | bytes 61448 | tf_op jit(solution)/shard_map/ppermute | solution.py:12
  42.7 1.3 %collective-permute-start.1 = (bf16[20,512]{0,1:T(8,128)(2,1)S(1)}, bf16[20,512]{0,1:T(8,128)(2,1)S(1)}, u32[]{:S(2)}, u32[]{:S(2)}) collective-permute-start(bf16[20,512]{0,1:T(8,128)(2,1)S(1)} %get-tuple-element.11), channel_id=1, source_target_pairs={{2,0},{3,1},{4,2},{5,3},{6,4},{7,5},{0,6},{1,7},{10,8},{11,9},{12,... | collective-permute-start | bytes 61448 | tf_op jit(solution)/shard_map/ppermute | solution.py:12
  44.0 0.1 copy.38
  44.1 0.0 collective-permute-done.6
  44.1 1.5 %collective-permute-start.2 = (bf16[20,512]{0,1:T(8,128)(2,1)S(1)}, bf16[20,512]{0,1:T(8,128)(2,1)S(1)}, u32[]{:S(2)}, u32[]{:S(2)}) collective-permute-start(bf16[20,512]{0,1:T(8,128)(2,1)S(1)} %get-tuple-element.10), channel_id=1, source_target_pairs={{1,0},{2,1},{3,2},{4,3},{5,4},{6,5},{7,6},{0,7},{9,8},{10,9},{11,1... | collective-permute-start | bytes 61448 | tf_op jit(solution)/shard_map/ppermute | solution.py:12
  45.6 0.0 collective-permute-done.7
  45.6 0.6 collective-permute-start.3
  46.2 0.0 collective-permute-done.8
  46.2 1.0 %collective-permute-start.4 = (bf16[20,512]{0,1:T(8,128)(2,1)S(1)}, bf16[20,512]{0,1:T(8,128)(2,1)S(1)}, u32[]{:S(2)}, u32[]{:S(2)}) collective-permute-start(bf16[20,512]{0,1:T(8,128)(2,1)S(1)} %get-tuple-element.7), channel_id=1, source_target_pairs={{6,0},{7,1},{0,2},{1,3},{2,4},{3,5},{4,6},{5,7},{14,8},{15,9},{8,1... | collective-permute-start | bytes 61448 | tf_op jit(solution)/shard_map/ppermute | solution.py:12
  47.3 0.0 collective-permute-done
  47.3 2.5 %collective-permute-start.5 = (bf16[20,512]{0,1:T(8,128)(2,1)S(1)}, bf16[20,512]{0,1:T(8,128)(2,1)S(1)}, u32[]{:S(2)}, u32[]{:S(2)}) collective-permute-start(bf16[20,512]{0,1:T(8,128)(2,1)S(1)} %get-tuple-element.6), channel_id=1, source_target_pairs={{5,0},{6,1},{7,2},{0,3},{1,4},{2,5},{3,6},{4,7},{13,8},{14,9},{15,... | collective-permute-start | bytes 61448 | tf_op jit(solution)/shard_map/ppermute | solution.py:12
  49.8 0.1 copy.35
  49.9 1.9 %collective-permute-done.1 = bf16[20,512]{0,1:T(8,128)(2,1)S(1)} collective-permute-done((bf16[20,512]{0,1:T(8,128)(2,1)S(1)}, bf16[20,512]{0,1:T(8,128)(2,1)S(1)}, u32[]{:S(2)}, u32[]{:S(2)}) %collective-permute-start.1) | collective-permute-done | bytes 20512 | tf_op jit(solution)/shard_map/ppermute | solution.py:12
  51.8 0.0 collective-permute-start.9
  51.8 0.1 copy.36
  51.9 0.2 collective-permute-done.2
  52.2 6.8 %collective-permute-start.10 = (bf16[14,512]{1,0:T(8,128)(2,1)S(1)}, bf16[14,512]{1,0:T(8,128)(2,1)S(1)}, u32[]{:S(2)}, u32[]{:S(2)}) collective-permute-start(bf16[14,512]{1,0:T(8,128)(2,1)S(1)} %get-tuple-element.14), channel_id=1, source_target_pairs={{6,0},{7,1},{0,2},{1,3},{2,4},{3,5},{4,6},{5,7},{14,8},{15,9},{8,1... | collective-permute-start | bytes 43016 | tf_op jit(solution)/shard_map/ppermute | solution.py:12
  59.0 0.1 copy.37
  59.1 0.0 collective-permute-done.3
  59.1 3.4 %collective-permute-start.11 = (bf16[14,512]{1,0:T(8,128)(2,1)S(1)}, bf16[14,512]{1,0:T(8,128)(2,1)S(1)}, u32[]{:S(2)}, u32[]{:S(2)}) collective-permute-start(bf16[14,512]{1,0:T(8,128)(2,1)S(1)} %get-tuple-element.13), channel_id=1, source_target_pairs={{5,0},{6,1},{7,2},{0,3},{1,4},{2,5},{3,6},{4,7},{13,8},{14,9},{15,... | collective-permute-start | bytes 43016 | tf_op jit(solution)/shard_map/ppermute | solution.py:12
  62.5 0.1 copy.39
  62.7 0.0 collective-permute-done.4
  62.7 0.1 copy.40
  62.8 0.0 collective-permute-done.5
  62.8 0.1 copy.41
  62.9 8.2 %all-gather = bf16[4,20,3584]{2,1,0:T(8,128)(2,1)S(1)} all-gather(bf16[1,20,3584]{2,1,0:T(8,128)(2,1)S(1)} %bitcast.30), channel_id=1, replica_groups=mesh['mem'=4,'reg'=8] {'mem'}, dimensions={0}, use_global_device_ids=true | all-gather | bytes 716800 | tf_op jit(solution)/shard_map/all_gather | solution.py:66
  71.2 0.1 reshape.156
  71.3 0.0 collective-permute-done.9
  71.3 0.0 collective-permute-done.10
  71.3 0.0 collective-permute-done.11
  71.4 0.1 slice_reduce_fusion.2
  71.4 4.3 %broadcast_multiply_fusion = bf16[80,12,3584]{2,1,0:T(8,128)(2,1)} fusion(bf16[12,3584]{1,0:T(8,128)(2,1)S(1)} %slice.105, bf16[80,3584]{1,0:T(8,128)(2,1)S(1)} %reshape.156), kind=kLoop, calls=%fused_computation.3 | loop fusion | flops 3440640 | bytes 7540736 | tf_op jit(solution)/shard_map/mul | solution.py:70
  75.8 11.2 %mul.68 = bf16[960,3584]{1,0:T(8,128)(2,1)} reshape(bf16[80,12,3584]{2,1,0:T(8,128)(2,1)} %broadcast_multiply_fusion) | data formatting | bytes 13762560 | tf_op jit(solution)/shard_map/mul | solution.py:70
  87.0 2.6 %fusion.8 = f32[1,240]{1,0:T(1,128)} fusion(bf16[960,3584]{1,0:T(8,128)(2,1)} %mul.68, s32[]{:T(128)S(6)} %select_n.60, bf16[14,3584]{1,0:T(8,128)(2,1)S(1)} %constant_dynamic-update-slice_fusion.7), kind=kOutput, calls=%fused_computation.17 | convolution fusion | flops 1720320 | bytes 1735620 | tf_op jit(solution)/shard_map/dot_general | solution.py:77
  89.6 6.5 %fusion.14 = f32[1,240,960]{2,1,0:T(8,128)} fusion(bf16[960,3584]{1,0:T(8,128)(2,1)} %mul.68, bf16[3584]{0:T(1024)(128)(2,1)S(1)} %slice_reduce_fusion.2, s32[]{:T(128)S(6)} %select_n.60), kind=kOutput, calls=%fused_computation.21 | convolution fusion | flops 1654947840 | bytes 9530372 | tf_op jit(solution)/shard_map/dot_general | solution.py:76
  (30 shorter events, 0.3 us)
Async XLA Ops:
  0.6 4.2 %copy-start = (bf16[256,20,127]{2,0,1:T(8,128)(2,1)S(1)}, bf16[256,20,127]{2,0,1:T(8,128)(2,1)}, u32[]{:S(2)}) copy-start(bf16[256,20,127]{2,0,1:T(8,128)(2,1)} %param.9) | copy-start | bytes 3901444
  5.8 1.6 %copy-start.4 = (s32[4096]{0:T(1024)S(1)}, s32[4096]{0:T(1024)}, u32[]{:S(2)}) copy-start(s32[4096]{0:T(1024)} %param.13) | copy-start | bytes 49156
  5.8 3.6 %copy-start.2 = (f32[4096]{0:T(1024)S(1)}, f32[4096]{0:T(1024)}, u32[]{:S(2)}) copy-start(f32[4096]{0:T(1024)} %param.12) | copy-start | bytes 49156
  7.4 4.0 %copy-start.3 = (f32[4096]{0:T(1024)S(1)}, f32[4096]{0:T(1024)}, u32[]{:S(2)}) copy-start(f32[4096]{0:T(1024)} %param.11) | copy-start | bytes 49156
  9.4 4.0 %copy-start.1 = (s32[1,7,512]{2,0,1:T(1,128)S(1)}, s32[1,7,512]{2,0,1:T(1,128)}, u32[]{:S(2)}) copy-start(s32[1,7,512]{2,0,1:T(1,128)} %param.15) | copy-start | bytes 43012
  28.9 3.1 %copy-start.5 = (f32[1,7,512]{2,0,1:T(1,128)S(1)}, f32[1,7,512]{2,0,1:T(1,128)}, u32[]{:S(2)}) copy-start(f32[1,7,512]{2,0,1:T(1,128)} %param.17) | copy-start | bytes 43012
  28.9 3.1 %copy-start.6 = (f32[127,12]{0,1:T(8,128)S(1)}, f32[127,12]{0,1:T(8,128)}, u32[]{:S(2)}) copy-start(f32[127,12]{0,1:T(8,128)} %param.14) | copy-start | bytes 18292
  32.9 11.2 %collective-permute-start.6 = (bf16[14,512]{1,0:T(8,128)(2,1)S(1)}, bf16[14,512]{1,0:T(8,128)(2,1)S(1)}, u32[]{:S(2)}, u32[]{:S(2)}) collective-permute-start(bf16[14,512]{1,0:T(8,128)(2,1)S(1)} %get-tuple-element.19), channel_id=1, source_target_pairs={{3,0},{4,1},{5,2},{6,3},{7,4},{0,5},{1,6},{2,7},{11,8},{12,9},{13,... | collective-permute-start | bytes 43016 | tf_op jit(solution)/shard_map/ppermute | solution.py:12
  38.0 7.6 %collective-permute-start.7 = (bf16[14,512]{1,0:T(8,128)(2,1)S(1)}, bf16[14,512]{1,0:T(8,128)(2,1)S(1)}, u32[]{:S(2)}, u32[]{:S(2)}) collective-permute-start(bf16[14,512]{1,0:T(8,128)(2,1)S(1)} %get-tuple-element.18), channel_id=1, source_target_pairs={{2,0},{3,1},{4,2},{5,3},{6,4},{7,5},{0,6},{1,7},{10,8},{11,9},{12,... | collective-permute-start | bytes 43016 | tf_op jit(solution)/shard_map/ppermute | solution.py:12
  39.3 6.9 %collective-permute-start.8 = (bf16[14,512]{1,0:T(8,128)(2,1)S(1)}, bf16[14,512]{1,0:T(8,128)(2,1)S(1)}, u32[]{:S(2)}, u32[]{:S(2)}) collective-permute-start(bf16[14,512]{1,0:T(8,128)(2,1)S(1)} %get-tuple-element.17), channel_id=1, source_target_pairs={{1,0},{2,1},{3,2},{4,3},{5,4},{6,5},{7,6},{0,7},{9,8},{10,9},{11,1... | collective-permute-start | bytes 43016 | tf_op jit(solution)/shard_map/ppermute | solution.py:12
  40.0 7.3 %collective-permute-start = (bf16[20,512]{0,1:T(8,128)(2,1)S(1)}, bf16[20,512]{0,1:T(8,128)(2,1)S(1)}, u32[]{:S(2)}, u32[]{:S(2)}) collective-permute-start(bf16[20,512]{0,1:T(8,128)(2,1)S(1)} %get-tuple-element.12), channel_id=1, source_target_pairs={{3,0},{4,1},{5,2},{6,3},{7,4},{0,5},{1,6},{2,7},{11,8},{12,9},{13,... | collective-permute-start | bytes 61448 | tf_op jit(solution)/shard_map/ppermute | solution.py:12
  42.7 9.1 %collective-permute-start.1 = (bf16[20,512]{0,1:T(8,128)(2,1)S(1)}, bf16[20,512]{0,1:T(8,128)(2,1)S(1)}, u32[]{:S(2)}, u32[]{:S(2)}) collective-permute-start(bf16[20,512]{0,1:T(8,128)(2,1)S(1)} %get-tuple-element.11), channel_id=1, source_target_pairs={{2,0},{3,1},{4,2},{5,3},{6,4},{7,5},{0,6},{1,7},{10,8},{11,9},{12,... | collective-permute-start | bytes 61448 | tf_op jit(solution)/shard_map/ppermute | solution.py:12
  44.1 8.0 %collective-permute-start.2 = (bf16[20,512]{0,1:T(8,128)(2,1)S(1)}, bf16[20,512]{0,1:T(8,128)(2,1)S(1)}, u32[]{:S(2)}, u32[]{:S(2)}) collective-permute-start(bf16[20,512]{0,1:T(8,128)(2,1)S(1)} %get-tuple-element.10), channel_id=1, source_target_pairs={{1,0},{2,1},{3,2},{4,3},{5,4},{6,5},{7,6},{0,7},{9,8},{10,9},{11,1... | collective-permute-start | bytes 61448 | tf_op jit(solution)/shard_map/ppermute | solution.py:12
  45.6 13.5 %collective-permute-start.3 = (bf16[20,512]{0,1:T(8,128)(2,1)S(1)}, bf16[20,512]{0,1:T(8,128)(2,1)S(1)}, u32[]{:S(2)}, u32[]{:S(2)}) collective-permute-start(bf16[20,512]{0,1:T(8,128)(2,1)S(1)} %get-tuple-element.8), channel_id=1, source_target_pairs={{7,0},{0,1},{1,2},{2,3},{3,4},{4,5},{5,6},{6,7},{15,8},{8,9},{9,10... | collective-permute-start | bytes 61448 | tf_op jit(solution)/shard_map/ppermute | solution.py:12
  46.2 16.4 %collective-permute-start.4 = (bf16[20,512]{0,1:T(8,128)(2,1)S(1)}, bf16[20,512]{0,1:T(8,128)(2,1)S(1)}, u32[]{:S(2)}, u32[]{:S(2)}) collective-permute-start(bf16[20,512]{0,1:T(8,128)(2,1)S(1)} %get-tuple-element.7), channel_id=1, source_target_pairs={{6,0},{7,1},{0,2},{1,3},{2,4},{3,5},{4,6},{5,7},{14,8},{15,9},{8,1... | collective-permute-start | bytes 61448 | tf_op jit(solution)/shard_map/ppermute | solution.py:12
  47.3 15.5 %collective-permute-start.5 = (bf16[20,512]{0,1:T(8,128)(2,1)S(1)}, bf16[20,512]{0,1:T(8,128)(2,1)S(1)}, u32[]{:S(2)}, u32[]{:S(2)}) collective-permute-start(bf16[20,512]{0,1:T(8,128)(2,1)S(1)} %get-tuple-element.6), channel_id=1, source_target_pairs={{5,0},{6,1},{7,2},{0,3},{1,4},{2,5},{3,6},{4,7},{13,8},{14,9},{15,... | collective-permute-start | bytes 61448 | tf_op jit(solution)/shard_map/ppermute | solution.py:12
  51.8 19.5 %collective-permute-start.9 = (bf16[14,512]{1,0:T(8,128)(2,1)S(1)}, bf16[14,512]{1,0:T(8,128)(2,1)S(1)}, u32[]{:S(2)}, u32[]{:S(2)}) collective-permute-start(bf16[14,512]{1,0:T(8,128)(2,1)S(1)} %get-tuple-element.15), channel_id=1, source_target_pairs={{7,0},{0,1},{1,2},{2,3},{3,4},{4,5},{5,6},{6,7},{15,8},{8,9},{9,10... | collective-permute-start | bytes 43016 | tf_op jit(solution)/shard_map/ppermute | solution.py:12
  52.2 19.1 %collective-permute-start.10 = (bf16[14,512]{1,0:T(8,128)(2,1)S(1)}, bf16[14,512]{1,0:T(8,128)(2,1)S(1)}, u32[]{:S(2)}, u32[]{:S(2)}) collective-permute-start(bf16[14,512]{1,0:T(8,128)(2,1)S(1)} %get-tuple-element.14), channel_id=1, source_target_pairs={{6,0},{7,1},{0,2},{1,3},{2,4},{3,5},{4,6},{5,7},{14,8},{15,9},{8,1... | collective-permute-start | bytes 43016 | tf_op jit(solution)/shard_map/ppermute | solution.py:12
  59.1 12.2 %collective-permute-start.11 = (bf16[14,512]{1,0:T(8,128)(2,1)S(1)}, bf16[14,512]{1,0:T(8,128)(2,1)S(1)}, u32[]{:S(2)}, u32[]{:S(2)}) collective-permute-start(bf16[14,512]{1,0:T(8,128)(2,1)S(1)} %get-tuple-element.13), channel_id=1, source_target_pairs={{5,0},{6,1},{7,2},{0,3},{1,4},{2,5},{3,6},{4,7},{13,8},{14,9},{15,... | collective-permute-start | bytes 43016 | tf_op jit(solution)/shard_map/ppermute | solution.py:12
where the time goes:
time: 96.6 us; the launch traced here: 96.1 us
  local copies, waits for them, and re-layouts  30.3 us (31%)
  starting transfers between devices  26.9 us (28%)
  other arithmetic  16.9 us (17%)
  matrix products  10.7 us (11%)
  blocking collectives  8.24 us (9%)
  waiting for transfers between devices  2.15 us (2%)
    ppermute x12, starting transfers between devices, from_behind(): return lax.ppermute(block, axis, route)  26.9 us
    mul x1, local copies, waits for them, and re-layouts, local(): modulated = region_pert[:, None, :] * slot_modes[None, :, :]  11.2 us
    all_gather x1, blocking collectives, local(): region_pert = lax.all_gather(region_pert, 'mem', axis=0, tiled=True)  8.24 us
    gather x1, local copies, waits for them, and re-layouts, local(): table_rows = jnp.take(table, picked, axis=0)  7.35 us
    dot_general x1, matrix products, local(): lax.dot_general(own_rows, weighted, contract, preferred_element_type=jnp....  6.53 us
    concatenate x1, other arithmetic, local(): jnp.concatenate([perturbed.astype(jnp.float32), obs_rinv[:, None], depart...  5.15 us
    mul x1, other arithmetic, local(): modulated = region_pert[:, None, :] * slot_modes[None, :, :]  4.33 us
    select_n x2, other arithmetic, local(): table_rows = jnp.take(table, picked, axis=0)  3.76 us
  transfers between devices with their start and end apart: 12, of which 2 were waited for; matrix products, arithmetic and copies ran while one was open for 1% of the time, Pallas kernels for 0%

commit v1 on v0

v1 whole, which is shorter than its diff:
```python
import functools

import jax
import jax.numpy as jnp
from jax import lax
from jax.experimental import pallas as pl
from jax.experimental.pallas import tpu as pltpu
from jax.sharding import PartitionSpec as P

ENS = 80
ROWS = 32
GROUP = 8
LO = 512
NT = (((1,), (1,)), ((), ()))
VMEM = pl.BlockSpec(memory_space=pltpu.VMEM)
SMEM = pl.BlockSpec(memory_space=pltpu.SMEM)
MESH = pl.DeviceIdType.MESH


def iota(shape, dim):
    return lax.broadcasted_iota(jnp.int32, shape, dim)


def split3(x):
    hi = x.astype(jnp.bfloat16).astype(jnp.float32)
    rest = x - hi
    mid = rest.astype(jnp.bfloat16).astype(jnp.float32)
    return hi, mid, rest - mid


def pick_kernel(
    prof, jac, dep, rinv, level, modes, rows, counts, taper, out, stack, extra, table, side, block
):
    cols, members, levels = prof.shape
    channels = jac.shape[1]
    blocks, capacity = rows.shape[1], rows.shape[2]
    lanes = GROUP * channels
    share = side.shape[0] // lax.axis_size("mem")
    me = lax.axis_index("mem")

    extra[...] = jnp.zeros_like(extra)
    for first, source in ((0, rinv), (3, dep)):
        for step, part in enumerate(split3(source[...])):
            extra[first + step : first + step + 1, :] = part
    extra[6:7, :] = level[...].astype(jnp.float32)

    lane_col = iota((ROWS, lanes), 1) // channels
    is_member = iota((ROWS, lanes), 0) < members

    def fill(hi, carry):
        for part in range(LO // lanes):
            group = hi * (LO // lanes) + part
            base = group * GROUP
            for c in range(GROUP):
                start = pl.multiple_of((base + c) * ROWS, ROWS)
                stack[pl.ds(start, members), :] = prof[base + c]
            left = stack[pl.ds(pl.multiple_of(base * ROWS, ROWS * GROUP), ROWS * GROUP), :]
            right = jac[pl.ds(base, GROUP)].reshape(lanes, levels)
            full = lax.dot_general(left, right, NT, preferred_element_type=jnp.float32)
            acc = jnp.zeros((ROWS, lanes), jnp.float32)
            for c in range(GROUP):
                keep = (lane_col == c) & is_member
                acc = jnp.where(keep, full[c * ROWS : (c + 1) * ROWS], acc)
            tail = extra[:, pl.ds(pl.multiple_of(group * lanes, lanes), lanes)]
            whole = jnp.concatenate([acc[: ROWS - 8], tail], axis=0)
            table[hi, :, part * lanes : (part + 1) * lanes] = whole.astype(jnp.bfloat16)
        return carry

    his = table.shape[0]
    lax.fori_loop(0, his, fill, 0)

    scaled = (modes[...] * ((ENS - 1) ** (-0.5))).astype(jnp.bfloat16)
    kinds = scaled.shape[1]
    side[...] = jnp.zeros_like(side)
    block[...] = jnp.zeros_like(block)
    for d in range(blocks):
        live = iota((1, capacity), 1) < counts[0, d]
        picked = jnp.where(live, rows[0, d : d + 1, :], 0)
        high, low = picked // LO, picked % LO
        hot = jnp.where(iota((LO, capacity), 0) == low, 1.0, 0.0).astype(jnp.bfloat16)
        found = jnp.dot(
            table[...].reshape(his * ROWS, LO), hot, preferred_element_type=jnp.float32
        )
        chosen = jnp.where(high == 0, found[:ROWS], 0.0)
        for h in range(1, his):
            chosen = jnp.where(high == h, found[h * ROWS : (h + 1) * ROWS], chosen)
        slot_rinv = chosen[24:25] + chosen[25:26] + chosen[26:27]
        slot_dep = chosen[27:28] + chosen[28:29] + chosen[29:30]
        slot_level = chosen[30:31].astype(jnp.int32)
        weight32 = jnp.where(live, slot_rinv * taper[0, d : d + 1, :], 0.0)
        level_hot = jnp.where(iota((levels, capacity), 0) == slot_level, 1.0, 0.0)
        side[0:1, :] = weight32
        side[1:2, :] = weight32 * slot_dep
        side[2 : 2 + kinds, :] = lax.dot_general(
            scaled,
            level_hot.astype(jnp.bfloat16),
            (((0,), (0,)), ((), ())),
            preferred_element_type=jnp.float32,
        )
        block[0:24, :] = chosen[0:24]
        for j in range(side.shape[0] // share):

            @pl.when(me == j)
            def _():
                block[members : members + share, :] = side[j * share : (j + 1) * share, :]

        out[d] = block[...].astype(jnp.bfloat16)


def share_kernel(mine, region, s_reg, r_reg, s_x, r_x, s_p, r_p, s_q, r_q, here):
    blocks = mine.shape[0]
    middle = blocks // 2
    n_mem, n_reg = lax.axis_size("mem"), lax.axis_size("reg")
    me, reg = lax.axis_index("mem"), lax.axis_index("reg")
    chips = n_mem // 2
    twin = me + 1 - 2 * (me % 2)
    order = [middle]
    for far in range(1, middle + 1):
        order += [middle - far, middle + far]

    def to_reg(d):
        return {"mem": me, "reg": lax.rem(reg + d - middle + n_reg, n_reg)}

    def peer(j):
        return {"mem": lax.rem(me + 2 * j, n_mem), "reg": reg}

    partner = {"mem": twin, "reg": reg}
    barrier = pltpu.get_barrier_semaphore()
    greeted = [to_reg(d) for d in order[1:]] + [partner] + [peer(j) for j in range(1, chips)]
    for device in greeted:
        pl.semaphore_signal(barrier, inc=1, device_id=device, device_id_type=MESH)
    own = pltpu.make_async_copy(mine.at[middle], region.at[middle, me], here)
    own.start()
    pl.semaphore_wait(barrier, len(greeted))

    def remote(src, dst, send, recv, device):
        return pltpu.make_async_remote_copy(
            src_ref=src, dst_ref=dst, send_sem=send, recv_sem=recv,
            device_id=device, device_id_type=MESH,
        )

    sends = []
    across = {}
    for d in order[1:]:
        across[d] = remote(mine.at[d], region.at[d, me], s_reg.at[d], r_reg.at[d], to_reg(d))
        across[d].start()
    hops = {}
    twins = []
    for d in order:
        src = mine.at[d]
        if d != middle:
            across[d].wait_recv()
            src = region.at[d, me]
        for j in range(1, chips):
            hops[d, j] = remote(
                src, region.at[d, me], s_x.at[d, j], r_x.at[d, j], peer(j)
            )
            hops[d, j].start()
        copy = remote(src, region.at[d, me], s_p.at[d], r_p.at[d], partner)
        copy.start()
        twins.append(copy)
    for d in order:
        for j in range(1, chips):
            hops[d, j].wait_recv()
            theirs = lax.rem(me - 2 * j + n_mem, n_mem)
            at = region.at[d, theirs]
            copy = remote(at, at, s_q.at[d, j], r_q.at[d, j], partner)
            copy.start()
            twins.append(copy)
    for copy in twins:
        copy.wait_recv()
    for copy in list(across.values()) + list(hops.values()) + twins:
        copy.wait_send()
    own.wait()


def gram_kernel(members, kinds, share, region, gram, depart, weighted, dep_acc):
    blocks, height, capacity = region.shape
    n_mem = height // ROWS
    own = members * kinds
    me = lax.axis_index("mem")
    row = iota((own, height), 0)
    col = iota((own, height), 1)
    member = ((row.astype(jnp.float32) + 0.5) * (1.0 / kinds)).astype(jnp.int32)
    line = row - member * kinds + 2

    def hot(mask):
        return jnp.where(mask, 1.0, 0.0).astype(jnp.bfloat16)

    spread = [hot(col == member + j * ROWS) for j in range(n_mem)]
    spread_own = hot(col == member + me * ROWS)
    mode_at = (line // share) * ROWS + members + line % share
    spread_mode = hot(col == mode_at)
    gram[...] = jnp.zeros_like(gram)
    dep_acc[...] = jnp.zeros_like(dep_acc)

    def times(left, right):
        return jnp.dot(left, right, preferred_element_type=jnp.float32)

    def step(d, carry):
        data = region[d]
        mode = times(spread_mode, data)
        top = data[16:32].astype(jnp.float32)
        weight = top[members - 16 : members - 15]
        dep = top[members - 15 : members - 14]
        z_own = (times(spread_own, data) * mode).astype(jnp.bfloat16)
        for j in range(n_mem):
            z = (times(spread[j], data) * mode).astype(jnp.bfloat16)
            weighted[j * own : (j + 1) * own, :] = (z.astype(jnp.float32) * weight).astype(
                jnp.bfloat16
            )
        gram[0] += lax.dot_general(z_own, weighted[...], NT, preferred_element_type=jnp.float32)
        dep8 = jnp.broadcast_to(dep, (16, capacity)).astype(jnp.bfloat16)
        dep_acc[...] += lax.dot_general(dep8, z_own, NT, preferred_element_type=jnp.float32)
        return carry

    lax.fori_loop(0, blocks, step, 0)
    depart[...] = dep_acc[0:1, :]


def local(
    profiles, jacobian, departure, obs_rinv, obs_level, vertical_modes, send_rows, counts, loc_taper
):
    cols, members, levels = profiles.shape
    channels = jacobian.shape[1]
    blocks, capacity = send_rows.shape[1], send_rows.shape[2]
    kinds = vertical_modes.shape[1]
    n_mem = lax.axis_size("mem")
    chips = n_mem // 2
    obs = cols * channels
    share = -(-(kinds + 2) // n_mem)
    mine = pl.pallas_call(
        pick_kernel,
        out_shape=jax.ShapeDtypeStruct((blocks, ROWS, capacity), jnp.bfloat16),
        in_specs=[VMEM] * 7 + [SMEM, VMEM],
        out_specs=VMEM,
        scratch_shapes=[
            pltpu.VMEM((cols * ROWS, levels), jnp.bfloat16),
            pltpu.VMEM((8, obs), jnp.float32),
            pltpu.VMEM((obs // LO, ROWS, LO), jnp.bfloat16),
            pltpu.VMEM((share * n_mem, capacity), jnp.float32),
            pltpu.VMEM((ROWS, capacity), jnp.float32),
        ],
        name="pick",
    )(
        profiles, jacobian, departure[None], obs_rinv[None], obs_level[None], vertical_modes,
        send_rows, counts, loc_taper,
    )
    dma = pltpu.SemaphoreType.DMA
    region = pl.pallas_call(
        share_kernel,
        out_shape=jax.ShapeDtypeStruct((blocks, n_mem, ROWS, capacity), jnp.bfloat16),
        in_specs=[VMEM],
        out_specs=VMEM,
        scratch_shapes=[dma((blocks,)), dma((blocks,)), dma((blocks, chips)), dma((blocks, chips)),
                        dma((blocks,)), dma((blocks,)), dma((blocks, chips)), dma((blocks, chips)),
                        dma],
        compiler_params=pltpu.CompilerParams(collective_id=0, has_side_effects=True),
        name="share",
    )(mine)
    own = members * kinds
    gram, depart = pl.pallas_call(
        functools.partial(gram_kernel, members, kinds, share),
        out_shape=(
            jax.ShapeDtypeStruct((1, own, own * n_mem), jnp.float32),
            jax.ShapeDtypeStruct((1, own), jnp.float32),
        ),
        in_specs=[VMEM],
        out_specs=(VMEM, VMEM),
        scratch_shapes=[
            pltpu.VMEM((own * n_mem, capacity), jnp.bfloat16),
            pltpu.VMEM((16, own), jnp.float32),
        ],
        name="gram",
    )(region.reshape(blocks, n_mem * ROWS, capacity))
    return gram, depart


def solution(mesh):
    in_specs = (
        P("reg", "mem", None),
        P("reg", None, None),
        P("reg"),
        P("reg"),
        P("reg"),
        P(),
        P("reg", None, None),
        P("reg", None),
        P("reg", None, None),
    )
    out_specs = (P("reg", "mem", None), P("reg", "mem"))
    return jax.shard_map(local, mesh=mesh, in_specs=in_specs, out_specs=out_specs, check_vma=False)
```

time: 96.6 us -> 44.5 us (0.46)
  Pallas kernels: 0 us -> 34 us
  starting transfers between devices: 26.9 us -> 0 us
  local copies, waits for them, and re-layouts: 30.3 us -> 9.4 us
  other arithmetic: 16.9 us -> 0 us
  matrix products: 10.7 us -> 0 us
  blocking collectives: 8.24 us -> 0 us
  waiting for transfers between devices: 2.15 us -> 0 us
    pallas_call x0 -> x3, Pallas kernels: none -> 34 us  [the longest x1 18.1 us: local(): pl.pallas_call(share_kernel, out_shape=jax.ShapeDtypeStruct((blocks, n_me...]
    ppermute x12 -> x0, starting transfers between devices: 26.9 us -> none  [from_behind(): return lax.ppermute(block, axis, route)]
    mul x1 -> x0, local copies, waits for them, and re-layouts: 11.2 us -> none  [local(): modulated = region_pert[:, None, :] * slot_modes[None, :, :]]
    dot_general x4 -> x0, matrix products: 10.7 us -> none  [the longest x1 6.53 us: local(): lax.dot_general(own_rows, weighted, contract, preferred_element_type=jnp....]
    all_gather x1 -> x0, blocking collectives: 8.24 us -> none  [local(): region_pert = lax.all_gather(region_pert, 'mem', axis=0, tiled=True)]
    gather x1 -> x0, local copies, waits for them, and re-layouts: 7.35 us -> none  [local(): table_rows = jnp.take(table, picked, axis=0)]
    unnamed x28 -> x7, local copies, waits for them, and re-layouts: 2.76 us -> 9.4 us
    broadcast_in_dim x3 -> x0, local copies, waits for them, and re-layouts: 5.94 us -> none  [the longest x1 2 us: local(): obs_level.astype(jnp.float32)[:, None]]
  transfers between devices with their start and end apart: 12 -> 0, of which waited for: 2 -> 0; matrix products, arithmetic and copies ran while one was open for 1% -> 0% of each run, Pallas kernels for 0% -> 0%
where the time goes in v1:
time: 44.5 us; the launch traced here: 44.1 us
  Pallas kernels  34 us (76%)
  local copies, waits for them, and re-layouts  9.4 us (21%)
  between operations  0.65 us (1%)
    pallas_call x1, Pallas kernels, local(): pl.pallas_call(share_kernel, out_shape=jax.ShapeDtypeStruct((blocks, n_me...  18.1 us
    unnamed x7, local copies, waits for them, and re-layouts  9.4 us
    pallas_call x1, Pallas kernels, local(): pl.pallas_call(functools.partial(gram_kernel, members, kinds, share), out...  8.17 us
    pallas_call x1, Pallas kernels, local(): pl.pallas_call(pick_kernel, out_shape=jax.ShapeDtypeStruct((blocks, ROWS,...  7.78 us

profile of v1, /device:TPU:0, one launch (start us, length us, event | category | flops | bytes accessed | tf_op | source)
XLA Modules:
  0.0 44.1 jit_solution(13877310794151869528)
XLA Ops:
  0.6 0.0 copy-start
  0.6 1.4 %copy.14.rows = s32[1,7,512]{2,1,0:T(8,128)} copy(s32[1,7,512]{2,0,1:T(1,128)} %param.15) | data formatting | bytes 28672 | tf_op args[6]
  2.1 1.3 %copy.15.taper = f32[1,7,512]{2,1,0:T(8,128)} copy(f32[1,7,512]{2,0,1:T(1,128)} %param.17) | data formatting | bytes 28672 | tf_op args[8]
  3.4 1.4 %copy.13.modes = f32[127,12]{1,0:T(8,128)} copy(f32[127,12]{0,1:T(8,128)} %param.14) | data formatting | bytes 12192 | tf_op args[5]
  4.8 3.2 %copy.12.jac = bf16[256,16,127]{2,1,0:T(8,128)(2,1)} copy(bf16[256,16,127]{0,1,2:T(8,128)(2,1)} %param.10) | data formatting | bytes 2080768 | tf_op args[1]
  8.0 0.0 copy-done
  8.0 2.0 %copy.11.prof = bf16[256,20,127]{2,1,0:T(8,128)(2,1)} copy(bf16[256,20,127]{2,0,1:T(8,128)(2,1)S(1)} %copy-done) | data formatting | bytes 2600960 | tf_op args[0]
  10.0 7.8 %pick.1.mine = bf16[7,32,512]{2,1,0:T(8,128)(2,1)} custom-call(bf16[256,20,127]{2,1,0:T(8,128)(2,1)} %copy.11.prof, bf16[256,16,127]{2,1,0:T(8,128)(2,1)} %copy.12.jac, f32[1,4096]{1,0:T(1,128)} %bitcast.5, f32[1,4096]{1,0:T(1,128)} %bitcast.6, s32[1,4096]{1,0:T(1,128)} %bitcast.7, f32[127,12]{1,0:T(8,128)} %copy.13.modes, s32[1,7,512]{2,1,0:T(8,128)} %copy.14.rows, ...), custom_call_target="tpu_custom_call" | custom-call | tf_op jit(solution)/shard_map/pick/pallas_call | solution.py:232
  17.8 18.1 %share.1 = bf16[7,4,32,512]{3,2,1,0:T(8,128)(2,1)} custom-call(bf16[7,32,512]{2,1,0:T(8,128)(2,1)} %pick.1.mine), custom_call_target="tpu_custom_call" | custom-call | tf_op jit(solution)/shard_map/share/pallas_call | solution.py:250
  35.9 8.2 %gram.1 = (f32[1,240,960]{2,1,0:T(8,128)}, f32[1,240]{1,0:T(1,128)}) custom-call(bf16[7,128,512]{2,1,0:T(8,128)(2,1)} %bitcast.4), custom_call_target="tpu_custom_call" | custom-call | tf_op jit(solution)/shard_map/gram/pallas_call | solution.py:262
Async XLA Ops:
  0.6 7.4 %copy-start = (bf16[256,20,127]{2,0,1:T(8,128)(2,1)S(1)}, bf16[256,20,127]{2,0,1:T(8,128)(2,1)}, u32[]{:S(2)}) copy-start(bf16[256,20,127]{2,0,1:T(8,128)(2,1)} %param.9) | copy-start | bytes 3901444

commit v2 on v1

v2 whole, which is shorter than its diff:
```python
import functools

import jax
import jax.numpy as jnp
from jax import lax
from jax.experimental import pallas as pl
from jax.experimental.pallas import tpu as pltpu
from jax.sharding import PartitionSpec as P

ENS = 80
LANE = 128
GROUP = 16
NT = (((1,), (1,)), ((), ()))
VMEM = pl.BlockSpec(memory_space=pltpu.VMEM)
SMEM = pl.BlockSpec(memory_space=pltpu.SMEM)
MESH = pl.DeviceIdType.MESH
LAG = 2


def iota(shape, dim):
    return lax.broadcasted_iota(jnp.int32, shape, dim)


def hot(mask):
    return jnp.where(mask, 1.0, 0.0).astype(jnp.bfloat16)


def times(left, right):
    return jnp.dot(left, right, preferred_element_type=jnp.float32)


def split3(x):
    hi = x.astype(jnp.bfloat16).astype(jnp.float32)
    rest = x - hi
    mid = rest.astype(jnp.bfloat16).astype(jnp.float32)
    return hi, mid, rest - mid


def pick_kernel(
    prof, jac, dep, rinv, level, modes, rows, counts, taper,
    out, wide, turned, extra, table, side, block,
):
    members, cols, levels = prof.shape
    channels = jac.shape[1]
    blocks, capacity = rows.shape[0], rows.shape[2]
    lanes = GROUP * channels
    his, height = table.shape[0], table.shape[1]
    share = side.shape[0] // lax.axis_size("mem")
    me = lax.axis_index("mem")

    depth = wide.shape[1] // channels
    for half in range(cols // LANE):
        part = jac[:, :, half * LANE : (half + 1) * LANE].reshape(levels * channels, LANE)
        wide[half, 0 : levels * channels, :] = part.astype(jnp.float32)
        for q in range(channels):
            plane = wide[half, pl.ds(q, depth, stride=channels), :]
            turned[q, half * LANE : (half + 1) * LANE, :] = plane.T[:, :levels].astype(jnp.bfloat16)

    extra[...] = jnp.zeros_like(extra)
    parts = split3(rinv[...]) + split3(dep[...]) + (level[...].astype(jnp.float32),)
    for k, part in enumerate(parts):
        for g in range(his):
            extra[g * 8 + k : g * 8 + k + 1, :] = part[:, g * lanes : (g + 1) * lanes]
    source, target = iota((lanes, lanes), 0), iota((lanes, lanes), 1)
    swap = hot(target == (source % channels) * GROUP + source // channels)
    extra[...] = times(extra[...].astype(jnp.bfloat16), swap)

    tall = members * GROUP
    diagonal = iota((tall, lanes), 0) % GROUP == iota((tall, lanes), 1) % GROUP
    fold = hot(iota((height, tall), 0) == iota((height, tall), 1) // GROUP)

    def fill(g, carry):
        first = pl.ds(pl.multiple_of(g * GROUP, GROUP), GROUP)
        left = prof[:, first, :].reshape(tall, levels)
        right = turned[:, first, :].reshape(lanes, levels)
        full = lax.dot_general(left, right, NT, preferred_element_type=jnp.float32)
        kept = jnp.where(diagonal, full, 0.0).astype(jnp.bfloat16)
        tail = extra[pl.ds(pl.multiple_of(g * 8, 8), 8), :]
        whole = jnp.concatenate([times(fold, kept)[: height - 8], tail], axis=0)
        table[g] = whole.astype(jnp.bfloat16)
        return carry

    lax.fori_loop(0, his, fill, 0, unroll=4)

    scaled = (modes[...] * ((ENS - 1) ** (-0.5))).astype(jnp.bfloat16)
    kinds = scaled.shape[0]
    side[...] = jnp.zeros_like(side)
    for d in range(blocks):
        live = iota((1, capacity), 1) < counts[0, d]
        picked = jnp.where(live, rows[d], 0)
        high = picked // lanes
        low = (picked % channels) * GROUP + (picked // channels) % GROUP
        found = times(
            table[...].reshape(his * height, lanes), hot(iota((lanes, capacity), 0) == low)
        )
        chosen = jnp.where(high == 0, found[:height], 0.0)
        for h in range(1, his):
            chosen = jnp.where(high == h, found[h * height : (h + 1) * height], chosen)
        x = height - 8
        slot_rinv = chosen[x : x + 1] + chosen[x + 1 : x + 2] + chosen[x + 2 : x + 3]
        slot_dep = chosen[x + 3 : x + 4] + chosen[x + 4 : x + 5] + chosen[x + 5 : x + 6]
        slot_level = chosen[x + 6 : x + 7].astype(jnp.int32)
        weight32 = jnp.where(live, slot_rinv * taper[d], 0.0)
        side[0:1, :] = weight32
        side[1:2, :] = weight32 * slot_dep
        side[2 : 2 + kinds, :] = times(scaled, hot(iota((levels, capacity), 0) == slot_level))
        block[0:members, :] = chosen[0:members]
        for j in range(side.shape[0] // share):

            @pl.when(me == j)
            def _():
                block[members : members + share, :] = side[j * share : (j + 1) * share, :]

        out[d] = block[...].astype(jnp.bfloat16)


def gram_kernel(
    members, kinds, share, mine, gram, depart,
    region, plain, weighted, dep_acc, s_reg, r_reg, s_x, r_x, s_p, r_p, s_q, r_q, here,
):
    blocks, height, capacity = mine.shape
    middle = blocks // 2
    n_mem, n_reg = lax.axis_size("mem"), lax.axis_size("reg")
    me, reg = lax.axis_index("mem"), lax.axis_index("reg")
    chips = n_mem // 2
    partner = {"mem": me + 1 - 2 * (me % 2), "reg": reg}

    def turn(k):
        return middle + ((k + 1) // 2) * (1 - 2 * (k % 2))

    def to_reg(d):
        return {"mem": me, "reg": lax.rem(reg + d - middle + n_reg, n_reg)}

    def peer(j):
        return {"mem": lax.rem(me + 2 * j, n_mem), "reg": reg}

    def remote(src, dst, send, recv, device):
        return pltpu.make_async_remote_copy(
            src_ref=src, dst_ref=dst, send_sem=send, recv_sem=recv,
            device_id=device, device_id_type=MESH,
        )

    def across(d):
        return remote(mine.at[d], region.at[d, me], s_reg.at[d], r_reg.at[d], to_reg(d))

    def hop(d, j):
        at = region.at[d, me]
        return remote(at, at, s_x.at[d, j], r_x.at[d, j], peer(j))

    def hand(d):
        at = region.at[d, me]
        return remote(at, at, s_p.at[d], r_p.at[d], partner)

    def relay(d, j):
        at = region.at[d, lax.rem(me - 2 * j + n_mem, n_mem)]
        return remote(at, at, s_q.at[d, j], r_q.at[d, j], partner)

    barrier = pltpu.get_barrier_semaphore()
    greeted = [to_reg(turn(k)) for k in range(1, blocks)] + [partner]
    greeted += [peer(j) for j in range(1, chips)]
    for device in greeted:
        pl.semaphore_signal(barrier, inc=1, device_id=device, device_id_type=MESH)
    own = pltpu.make_async_copy(mine.at[middle], region.at[middle, me], here)
    own.start()
    gram[...] = jnp.zeros_like(gram)
    dep_acc[...] = jnp.zeros_like(dep_acc)
    size = members * kinds
    row, col = iota((size, height), 0), iota((size, height), 1)
    spread = hot(col == row // kinds)
    period = 4 * kinds
    line = iota((period, height), 0) % kinds + 2
    spot = iota((period, height), 1)
    spread_mode = [
        hot((line // share == j) & (spot == members + line % share)) for j in range(n_mem)
    ]
    pl.semaphore_wait(barrier, len(greeted))
    for k in range(1, blocks):
        across(turn(k)).start()
    own.wait()

    def forward(k):
        d = turn(k)

        @pl.when(k > 0)
        def _():
            across(d).wait_recv()

        for j in range(1, chips):
            hop(d, j).start()
        hand(d).start()

    def pass_on(k):
        d = turn(k)
        for j in range(1, chips):
            hop(d, j).wait_recv()
            relay(d, j).start()

    def multiply(k):
        d = turn(k)
        hand(d).wait_recv()
        for j in range(1, chips):
            relay(d, j).wait_recv()
        mode = times(spread_mode[0], region[d, 0])
        for j in range(1, n_mem):
            mode += times(spread_mode[j], region[d, j])
        mode = jnp.concatenate([mode] * (size // period), axis=0)
        rows = region[d, 0].astype(jnp.float32)
        weight, dep = rows[members : members + 1], rows[members + 1 : members + 2]
        for j in range(n_mem):
            z = (times(spread, region[d, j]) * mode).astype(jnp.bfloat16)
            plain[j] = z
            weighted[j * size : (j + 1) * size, :] = (z.astype(jnp.float32) * weight).astype(
                jnp.bfloat16
            )
        z_own = plain[me]
        gram[0] += lax.dot_general(z_own, weighted[...], NT, preferred_element_type=jnp.float32)
        dep16 = jnp.broadcast_to(dep, (16, capacity)).astype(jnp.bfloat16)
        dep_acc[...] += lax.dot_general(dep16, z_own, NT, preferred_element_type=jnp.float32)

    def step(k, carry):
        @pl.when(k < blocks)
        def _():
            forward(k)

        @pl.when((k >= LAG) & (k < blocks + LAG))
        def _():
            pass_on(k - LAG)

        @pl.when(k >= 2 * LAG)
        def _():
            multiply(k - 2 * LAG)

        return carry

    lax.fori_loop(0, blocks + 2 * LAG, step, 0)
    for k in range(blocks):
        d = turn(k)
        if k > 0:
            across(d).wait_send()
        hand(d).wait_send()
        for j in range(1, chips):
            hop(d, j).wait_send()
            relay(d, j).wait_send()
    depart[...] = dep_acc[0:1, :]


def local(
    profiles, jacobian, departure, obs_rinv, obs_level, vertical_modes, send_rows, counts, loc_taper
):
    cols, members, levels = profiles.shape
    channels = jacobian.shape[1]
    blocks, capacity = send_rows.shape[1], send_rows.shape[2]
    kinds = vertical_modes.shape[1]
    n_mem = lax.axis_size("mem")
    chips = n_mem // 2
    share = -(-(kinds + 2) // n_mem)
    height = members + share
    mine = pl.pallas_call(
        pick_kernel,
        out_shape=jax.ShapeDtypeStruct((blocks, height, capacity), jnp.bfloat16),
        in_specs=[VMEM] * 7 + [SMEM, VMEM],
        out_specs=VMEM,
        scratch_shapes=[
            pltpu.VMEM((cols // LANE, -(-levels // LANE) * LANE * channels, LANE), jnp.float32),
            pltpu.VMEM((channels, cols, levels), jnp.bfloat16),
            pltpu.VMEM((cols // GROUP * 8, GROUP * channels), jnp.float32),
            pltpu.VMEM((cols // GROUP, 32, GROUP * channels), jnp.bfloat16),
            pltpu.VMEM((share * n_mem, capacity), jnp.float32),
            pltpu.VMEM((height, capacity), jnp.float32),
        ],
        name="pick",
    )(
        profiles.transpose(1, 0, 2), jacobian.transpose(2, 1, 0),
        departure[None], obs_rinv[None], obs_level[None], vertical_modes.T,
        send_rows.transpose(1, 0, 2), counts, loc_taper.transpose(1, 0, 2),
    )
    dma = pltpu.SemaphoreType.DMA
    own = members * kinds
    one, two = dma((blocks,)), dma((blocks, chips))
    gram, depart = pl.pallas_call(
        functools.partial(gram_kernel, members, kinds, share),
        out_shape=(
            jax.ShapeDtypeStruct((1, own, own * n_mem), jnp.float32),
            jax.ShapeDtypeStruct((1, own), jnp.float32),
        ),
        in_specs=[VMEM],
        out_specs=(VMEM, VMEM),
        scratch_shapes=[
            pltpu.VMEM((blocks, n_mem, height, capacity), jnp.bfloat16),
            pltpu.VMEM((n_mem, own, capacity), jnp.bfloat16),
            pltpu.VMEM((own * n_mem, capacity), jnp.bfloat16),
            pltpu.VMEM((16, own), jnp.float32),
            one, one, two, two, one, one, two, two, dma,
        ],
        compiler_params=pltpu.CompilerParams(collective_id=0, has_side_effects=True),
        name="gram",
    )(mine)
    return gram, depart


def solution(mesh):
    in_specs = (
        P("reg", "mem", None),
        P("reg", None, None),
        P("reg"),
        P("reg"),
        P("reg"),
        P(),
        P("reg", None, None),
        P("reg", None),
        P("reg", None, None),
    )
    out_specs = (P("reg", "mem", None), P("reg", "mem"))
    return jax.shard_map(local, mesh=mesh, in_specs=in_specs, out_specs=out_specs, check_vma=False)
```

time: 44.5 us -> 36.7 us (0.82)
  local copies, waits for them, and re-layouts: 9.4 us -> 2.81 us
  Pallas kernels: 34 us -> 33.1 us
    pallas_call x2 -> x1, Pallas kernels: 25.9 us -> 10.9 us  [local(): pl.pallas_call(pick_kernel, out_shape=jax.ShapeDtypeStruct((blocks, heigh...]
    pallas_call x1, Pallas kernels: 8.17 us -> 22.2 us  [local(): pl.pallas_call(functools.partial(gram_kernel, members, kinds, share), out...]
    unnamed x7 -> x4, local copies, waits for them, and re-layouts: 9.4 us -> 2.81 us
where the time goes in v2:
time: 36.7 us; the launch traced here: 36.5 us
  Pallas kernels  33.1 us (90%)
  local copies, waits for them, and re-layouts  2.81 us (8%)
  between operations  0.65 us (2%)
    pallas_call x1, Pallas kernels, local(): pl.pallas_call(functools.partial(gram_kernel, members, kinds, share), out...  22.2 us
    pallas_call x1, Pallas kernels, local(): pl.pallas_call(pick_kernel, out_shape=jax.ShapeDtypeStruct((blocks, heigh...  10.9 us
    unnamed x4, local copies, waits for them, and re-layouts  2.81 us

profile of v2, /device:TPU:0, one launch (start us, length us, event | category | flops | bytes accessed | tf_op | source)
XLA Modules:
  0.0 36.5 jit_solution(15803930885295701750)
XLA Ops:
  0.6 10.9 %pick.1.mine = bf16[7,24,512]{2,1,0:T(8,128)(2,1)} custom-call(bf16[20,256,127]{2,1,0:T(8,128)(2,1)} %bitcast.8, bf16[127,16,256]{2,1,0:T(8,128)(2,1)} %bitcast.9, f32[1,4096]{1,0:T(1,128)} %bitcast.10, f32[1,4096]{1,0:T(1,128)} %bitcast.11, s32[1,4096]{1,0:T(1,128)} %bitcast.12, f32[12,127]{1,0:T(8,128)} %bitcast.15, s32[7,1,512]{2,1,0:T(1,128)} %bitcast.13, ...), custom_call_target="tpu_custom_call" | custom-call | tf_op jit(solution)/shard_map/pick/pallas_call | solution.py:258
  11.5 22.2 %gram.1 = (f32[1,240,960]{2,1,0:T(8,128)}, f32[1,240]{1,0:T(1,128)}) custom-call(bf16[7,24,512]{2,1,0:T(8,128)(2,1)} %pick.1.mine), custom_call_target="tpu_custom_call" | custom-call | tf_op jit(solution)/shard_map/gram/pallas_call | solution.py:280
  33.7 0.0 copy-start
  33.7 2.2 %copy.13 = f32[1,240,960]{2,1,0:T(8,128)} copy(f32[1,240,960]{2,1,0:T(8,128)} %get-tuple-element.4) | data formatting | bytes 1843200
  36.0 0.0 copy-done
  36.0 0.6 %copy.14 = f32[1,240]{1,0:T(1,128)} copy(f32[1,240]{1,0:T(1,128)S(1)} %copy-done) | data formatting | bytes 1920
Async XLA Ops:
  33.7 2.3 %copy-start = (f32[1,240]{1,0:T(1,128)S(1)}, f32[1,240]{1,0:T(1,128)}, u32[]{:S(2)}) copy-start(f32[1,240]{1,0:T(1,128)} %get-tuple-element.5) | copy-start | bytes 2884

commit v3 on v2

--- a/solution.py
+++ b/solution.py
@@ -36,8 +36,8 @@
     return hi, mid, rest - mid
 
 
-def pick_kernel(
-    prof, jac, dep, rinv, level, modes, rows, counts, taper,
+def pick(
+    order, ready, prof, jac, dep, rinv, level, modes, rows, counts, taper,
     out, wide, turned, extra, table, side, block,
 ):
     members, cols, levels = prof.shape
@@ -85,7 +85,7 @@
     scaled = (modes[...] * ((ENS - 1) ** (-0.5))).astype(jnp.bfloat16)
     kinds = scaled.shape[0]
     side[...] = jnp.zeros_like(side)
-    for d in range(blocks):
+    for k, d in enumerate(order):
         live = iota((1, capacity), 1) < counts[0, d]
         picked = jnp.where(live, rows[d], 0)
         high = picked // lanes
@@ -112,11 +112,12 @@
                 block[members : members + share, :] = side[j * share : (j + 1) * share, :]
 
         out[d] = block[...].astype(jnp.bfloat16)
+        ready(k)
 
 
 def gram_kernel(
-    members, kinds, share, mine, gram, depart,
-    region, plain, weighted, dep_acc, s_reg, r_reg, s_x, r_x, s_p, r_p, s_q, r_q, here,
+    members, kinds, share, prof, jac, dep, rinv, level, modes, rows, counts, taper, gram, depart,
+    wide, turned, extra, table, side, block, mine, region, plain, weighted, dep_acc, s_reg, r_reg, s_x, r_x, s_p, r_p, s_q, r_q,
 ):
     blocks, height, capacity = mine.shape
     middle = blocks // 2
@@ -126,6 +127,7 @@
     partner = {"mem": me + 1 - 2 * (me % 2), "reg": reg}
 
     def turn(k):
+        k = blocks - 1 - k
         return middle + ((k + 1) // 2) * (1 - 2 * (k % 2))
 
     def to_reg(d):
@@ -156,12 +158,23 @@
         return remote(at, at, s_q.at[d, j], r_q.at[d, j], partner)
 
     barrier = pltpu.get_barrier_semaphore()
-    greeted = [to_reg(turn(k)) for k in range(1, blocks)] + [partner]
+    greeted = [to_reg(turn(k)) for k in range(blocks - 1)] + [partner]
     greeted += [peer(j) for j in range(1, chips)]
     for device in greeted:
         pl.semaphore_signal(barrier, inc=1, device_id=device, device_id_type=MESH)
-    own = pltpu.make_async_copy(mine.at[middle], region.at[middle, me], here)
-    own.start()
+
+    def ready(k):
+        if k == blocks - 1:
+            region[middle, me] = mine[middle]
+        if k == 1:
+            pl.semaphore_wait(barrier, len(greeted))
+        if k > 0:
+            across(turn(k - 1)).start()
+
+    pick(
+        [turn(k) for k in range(blocks)], ready, prof, jac, dep, rinv, level, modes, rows, counts,
+        taper, mine, wide, turned, extra, table, side, block,
+    )
     gram[...] = jnp.zeros_like(gram)
     dep_acc[...] = jnp.zeros_like(dep_acc)
     size = members * kinds
@@ -173,15 +186,11 @@
     spread_mode = [
         hot((line // share == j) & (spot == members + line % share)) for j in range(n_mem)
     ]
-    pl.semaphore_wait(barrier, len(greeted))
-    for k in range(1, blocks):
-        across(turn(k)).start()
-    own.wait()
 
     def forward(k):
         d = turn(k)
 
-        @pl.when(k > 0)
+        @pl.when(k < blocks - 1)
         def _():
             across(d).wait_recv()
 
@@ -204,8 +213,8 @@
         for j in range(1, n_mem):
             mode += times(spread_mode[j], region[d, j])
         mode = jnp.concatenate([mode] * (size // period), axis=0)
-        rows = region[d, 0].astype(jnp.float32)
-        weight, dep = rows[members : members + 1], rows[members + 1 : members + 2]
+        first = region[d, 0].astype(jnp.float32)
+        weight, depw = first[members : members + 1], first[members + 1 : members + 2]
         for j in range(n_mem):
             z = (times(spread, region[d, j]) * mode).astype(jnp.bfloat16)
             plain[j] = z
@@ -214,7 +223,7 @@
             )
         z_own = plain[me]
         gram[0] += lax.dot_general(z_own, weighted[...], NT, preferred_element_type=jnp.float32)
-        dep16 = jnp.broadcast_to(dep, (16, capacity)).astype(jnp.bfloat16)
+        dep16 = jnp.broadcast_to(depw, (16, capacity)).astype(jnp.bfloat16)
         dep_acc[...] += lax.dot_general(dep16, z_own, NT, preferred_element_type=jnp.float32)
 
     def step(k, carry):
@@ -235,7 +244,7 @@
     lax.fori_loop(0, blocks + 2 * LAG, step, 0)
     for k in range(blocks):
         d = turn(k)
-        if k > 0:
+        if k < blocks - 1:
             across(d).wait_send()
         hand(d).wait_send()
         for j in range(1, chips):
@@ -255,25 +264,6 @@
     chips = n_mem // 2
     share = -(-(kinds + 2) // n_mem)
     height = members + share
-    mine = pl.pallas_call(
-        pick_kernel,
-        out_shape=jax.ShapeDtypeStruct((blocks, height, capacity), jnp.bfloat16),
-        in_specs=[VMEM] * 7 + [SMEM, VMEM],
-        out_specs=VMEM,
-        scratch_shapes=[
-            pltpu.VMEM((cols // LANE, -(-levels // LANE) * LANE * channels, LANE), jnp.float32),
-            pltpu.VMEM((channels, cols, levels), jnp.bfloat16),
-            pltpu.VMEM((cols // GROUP * 8, GROUP * channels), jnp.float32),
-            pltpu.VMEM((cols // GROUP, 32, GROUP * channels), jnp.bfloat16),
-            pltpu.VMEM((share * n_mem, capacity), jnp.float32),
-            pltpu.VMEM((height, capacity), jnp.float32),
-        ],
-        name="pick",
-    )(
-        profiles.transpose(1, 0, 2), jacobian.transpose(2, 1, 0),
-        departure[None], obs_rinv[None], obs_level[None], vertical_modes.T,
-        send_rows.transpose(1, 0, 2), counts, loc_taper.transpose(1, 0, 2),
-    )
     dma = pltpu.SemaphoreType.DMA
     own = members * kinds
     one, two = dma((blocks,)), dma((blocks, chips))
@@ -283,18 +273,29 @@
             jax.ShapeDtypeStruct((1, own, own * n_mem), jnp.float32),
             jax.ShapeDtypeStruct((1, own), jnp.float32),
         ),
-        in_specs=[VMEM],
+        in_specs=[VMEM] * 7 + [SMEM, VMEM],
         out_specs=(VMEM, VMEM),
         scratch_shapes=[
+            pltpu.VMEM((cols // LANE, -(-levels // LANE) * LANE * channels, LANE), jnp.float32),
+            pltpu.VMEM((channels, cols, levels), jnp.bfloat16),
+            pltpu.VMEM((cols // GROUP * 8, GROUP * channels), jnp.float32),
+            pltpu.VMEM((cols // GROUP, 32, GROUP * channels), jnp.bfloat16),
+            pltpu.VMEM((share * n_mem, capacity), jnp.float32),
+            pltpu.VMEM((height, capacity), jnp.float32),
+            pltpu.VMEM((blocks, height, capacity), jnp.bfloat16),
             pltpu.VMEM((blocks, n_mem, height, capacity), jnp.bfloat16),
             pltpu.VMEM((n_mem, own, capacity), jnp.bfloat16),
             pltpu.VMEM((own * n_mem, capacity), jnp.bfloat16),
             pltpu.VMEM((16, own), jnp.float32),
-            one, one, two, two, one, one, two, two, dma,
+            one, one, two, two, one, one, two, two,
         ],
         compiler_params=pltpu.CompilerParams(collective_id=0, has_side_effects=True),
         name="gram",
-    )(mine)
+    )(
+        profiles.transpose(1, 0, 2), jacobian.transpose(2, 1, 0),
+        departure[None], obs_rinv[None], obs_level[None], vertical_modes.T,
+        send_rows.transpose(1, 0, 2), counts, loc_taper.transpose(1, 0, 2),
+    )
     return gram, depart
 
 

time: 36.7 us -> 32.9 us (0.90)
  Pallas kernels: 33.1 us -> 29.3 us
    pallas_call x1 -> x0, Pallas kernels: 10.9 us -> none  [local(): pl.pallas_call(pick_kernel, out_shape=jax.ShapeDtypeStruct((blocks, heigh...]
    pallas_call x1, Pallas kernels: 22.2 us -> 29.3 us  [local(): pl.pallas_call(functools.partial(gram_kernel, members, kinds, share), out...]
where the time goes in v3:
time: 32.9 us; the launch traced here: 32.7 us
  Pallas kernels  29.3 us (89%)
  local copies, waits for them, and re-layouts  2.81 us (9%)
  between operations  0.65 us (2%)
    pallas_call x1, Pallas kernels, local(): pl.pallas_call(functools.partial(gram_kernel, members, kinds, share), out...  29.3 us
    unnamed x4, local copies, waits for them, and re-layouts  2.81 us

profile of v3, /device:TPU:0, one launch (start us, length us, event | category | flops | bytes accessed | tf_op | source)
XLA Modules:
  0.0 32.7 jit_solution(11940300204337876274)
XLA Ops:
  0.6 29.3 %gram.1 = (f32[1,240,960]{2,1,0:T(8,128)}, f32[1,240]{1,0:T(1,128)}) custom-call(bf16[20,256,127]{2,1,0:T(8,128)(2,1)} %bitcast.8, bf16[127,16,256]{2,1,0:T(8,128)(2,1)} %bitcast.9, f32[1,4096]{1,0:T(1,128)} %bitcast.10, f32[1,4096]{1,0:T(1,128)} %bitcast.11, s32[1,4096]{1,0:T(1,128)} %bitcast.12, f32[12,127]{1,0:T(8,128)} %bitcast.15, ...), custom_call_target="tpu_custom_call" | custom-call | tf_op jit(solution)/shard_map/gram/pallas_call | solution.py:270
  29.9 0.0 copy-start
  29.9 2.2 %copy.13 = f32[1,240,960]{2,1,0:T(8,128)} copy(f32[1,240,960]{2,1,0:T(8,128)} %get-tuple-element.4) | data formatting | bytes 1843200
  32.2 0.0 copy-done
  32.2 0.6 %copy.14 = f32[1,240]{1,0:T(1,128)} copy(f32[1,240]{1,0:T(1,128)S(1)} %copy-done) | data formatting | bytes 1920
Async XLA Ops:
  29.9 2.3 %copy-start = (f32[1,240]{1,0:T(1,128)S(1)}, f32[1,240]{1,0:T(1,128)}, u32[]{:S(2)}) copy-start(f32[1,240]{1,0:T(1,128)} %get-tuple-element.5) | copy-start | bytes 2884
